TPU v7x, 512 devices: a 4x2x32 block of a 4x8x32 slice. The times are simulated.
512 devices in a mesh: groups: 2 (over y), row: 128 (over z, x), col: 2 (over core).
Axes of the slice: x: 4, y: 2, z: 32, core: 2. Of those that a mesh axis runs over, the one named last changes fastest.
The devices are a block of a 4x8x32 slice.
Arguments:
- pair_act: bfloat16 [1024, 512, 128], P(('groups', 'row'), 'col'), parts along dimension 0, may hold values from -6 to 6
- in_gain: float32 [128], replicated, may hold values from 0.5 to 1.5
- in_shift: float32 [128], replicated, may hold values from -1 to 1
- left_weight: bfloat16 [128, 256], replicated, may hold values from -0.5 to 0.5
- left_bias: float32 [256], replicated, may hold values from -3 to 3
- right_weight: bfloat16 [128, 256], replicated, may hold values from -0.5 to 0.5
- right_bias: float32 [256], replicated, may hold values from -3 to 3
- gate_weight: bfloat16 [128, 128], replicated, may hold values from -0.5 to 0.5
- gate_bias: float32 [128], replicated, may hold values from -4 to 4
- out_gain: float32 [128], replicated, may hold values from 0.8 to 1.2
- out_shift: float32 [128], replicated, may hold values from -3 to 3
- out_weight: bfloat16 [128, 128], replicated, may hold values from -1 to 1
- out_bias: float32 [128], replicated, may hold values from -3 to 3
Outputs:
- update: bfloat16 [1024, 512, 128], P(('groups', 'row'), 'col'), parts along dimension 0
There are 2 independent parts, one for each index of `groups`. A program takes and returns all parts, laid end to end along the dimension named above; an argument that names none is the same for every part. Nothing has to cross between parts.
All inputs are finite; a program needn't handle non-finite values.
Results may differ from a plain program's by a relative error of at most 0.0061.
Values may be sent and summed in bfloat16 or wider, within the bound.
No kernel may reach another device: no remote copies, remote signals or barrier semaphores. Data moves between devices by JAX's collectives and lax.ppermute only.
A program may use at most 64 MiB of HBM per device.

v0:
```python
import jax
import jax.numpy as jnp
from jax import lax
from jax.sharding import PartitionSpec as P


def sent_together(arrays, axis, split_dim, concat_dim, along):
    both = jnp.concatenate(arrays, axis=along)
    filled, at, outs = (
        lax.all_to_all(both, axis, split_axis=split_dim, concat_axis=concat_dim, tiled=True),
        0,
        [],
    )
    for a in arrays:
        outs.append(lax.slice_in_dim(filled, at, at + a.shape[along], axis=along))
        at += a.shape[along]
    return tuple(outs)


def split_up(shard, dim, length):
    before, after = (shard.shape[:dim], shard.shape[dim + 1 :])
    return jnp.moveaxis(shard.reshape(*before, length, -1, *after), dim, 0)


def summed_on_arrival(shard, axis, dim):
    length = lax.axis_size(axis)
    tiles = lax.all_to_all(split_up(shard, dim, length), axis, 0, 0, tiled=True)
    return jnp.sum(tiles, axis=0)


def layer_norm(values, gain, shift, axis):
    center = values - jnp.mean(values, axis=axis, keepdims=True)
    spread = jnp.mean(center * center, axis=axis, keepdims=True)
    return center * lax.rsqrt(spread + 1e-05) * gain + shift


def edge_projection(normed, weight, bias, hidden):
    joined = (
        jnp.einsum("rkc,cd->drk", normed, weight, preferred_element_type=jnp.float32)
        + bias[:, None, None]
    )
    return (jax.nn.sigmoid(joined[:hidden]) * joined[hidden:]).astype(jnp.bfloat16)


def per_device(
    pair_act,
    in_gain,
    in_shift,
    left_weight,
    left_bias,
    right_weight,
    right_bias,
    gate_weight,
    gate_bias,
    out_gain,
    out_shift,
    out_weight,
    out_bias,
):
    hidden = left_weight.shape[1] // 2
    normed = layer_norm(pair_act.astype(jnp.float32), in_gain, in_shift, 2).astype(jnp.bfloat16)
    left_edge = edge_projection(normed, left_weight, left_bias, hidden)
    right_edge = edge_projection(normed, right_weight, right_bias, hidden)
    gate = jax.nn.sigmoid(
        jnp.einsum("rkc,cd->rkd", normed, gate_weight, preferred_element_type=jnp.float32)
        + gate_bias
    )
    left_chan, right_chan = sent_together((left_edge, right_edge), "row", 0, 1, 2)
    partial_sums = jnp.einsum(
        "cik,cjk->cij", left_chan, right_chan, preferred_element_type=jnp.float32
    )
    summed = summed_on_arrival(partial_sums, "col", 2)
    triangle_chan = summed.astype(jnp.bfloat16)
    triangle = lax.all_to_all(triangle_chan, "row", split_axis=1, concat_axis=0, tiled=True)
    mixed = layer_norm(
        triangle.astype(jnp.float32), out_gain[:, None, None], out_shift[:, None, None], 0
    ).astype(jnp.bfloat16)
    projected = (
        jnp.einsum("cij,cd->ijd", mixed, out_weight, preferred_element_type=jnp.float32) + out_bias
    )
    return (gate * projected).astype(jnp.bfloat16)


def solution(mesh):
    in_specs = (
        P(("groups", "row"), "col", None),
        P(),
        P(),
        P(),
        P(),
        P(),
        P(),
        P(),
        P(),
        P(),
        P(),
        P(),
        P(),
    )
    out_specs = P(("groups", "row"), "col", None)
    return jax.shard_map(
        per_device, mesh=mesh, in_specs=in_specs, out_specs=out_specs, check_vma=False
    )
```

profile of v0, /device:TPU:38, one launch (start us, length us, event | category | flops | bytes accessed | tf_op | source)
XLA Modules:
  0.0 181.3 jit_solution(12232461656241570481)
XLA Ops:
  0.0 0.0 copy-start
  0.0 0.0 copy-start.1
  0.0 1.2 convert_reduce_fusion
  1.2 0.0 copy-done.1
  1.2 0.4 fusion.10
  1.6 0.0 copy-start.4
  1.6 0.0 copy-start.5
  1.6 0.0 copy-start.6
  1.6 0.0 copy-done
  1.6 0.6 copy-done.4
  2.2 0.0 copy-done.5
  2.3 0.0 copy-done.6
  2.3 0.0 copy-start.7
  2.3 0.5 fusion.1
  2.8 0.4 copy-done.2
  3.1 0.0 copy-done.7
  3.1 0.5 fusion
  3.6 0.3 fusion.14
  3.9 0.4 copy.19
  4.3 112.5 %all_to_all.26 = bf16[128,4,512]{2,1,0:T(4,128)(2,1)S(1)} all-to-all(bf16[128,4,512]{2,1,0:T(4,128)(2,1)S(1)} %copy.19), channel_id=1, replica_groups=mesh['groups'=2,'row'=128,'col'=2] {'row'}, dimensions={0} | all-to-all | bytes 1048576 | tf_op jit(solution)/shard_map/all_to_all | solution.py:10
  116.9 0.1 all_to_all.9
  117.0 0.3 convolution_bitcast_fusion
  117.4 4.6 %all_to_all.27 = f32[2,1,512,256]{3,2,1,0:T(8,128)S(1)} all-to-all(f32[2,1,512,256]{3,2,1,0:T(8,128)S(1)} %convolution_bitcast_fusion), channel_id=1, replica_groups=mesh['groups'=2,'row'=128,'col'=2] {'col'}, dimensions={0} | all-to-all | bytes 2097152 | tf_op jit(solution)/shard_map/all_to_all | solution.py:27
  122.0 0.1 reduce_sum.47
  122.0 0.4 copy.27
  122.4 0.5 broadcast.71
  123.0 2.2 %reduce.3 = bf16[512,256]{1,0:T(8,128)(2,1)S(1)} reduce(bf16[512,1,256]{2,1,0:T(2,128)(2,1)S(1)} %bitcast.36, bf16[]{:T(256)} %broadcast.71), dimensions={1}, to_apply=%bitcast.35.reduce_sub_computation | reduce | bytes 524290
  125.2 0.2 reshape.74
  125.3 50.3 %all_to_all.28 = bf16[128,2,512]{2,1,0:T(2,128)(2,1)S(1)} all-to-all(bf16[128,2,512]{2,1,0:T(2,128)(2,1)S(1)} %reshape.74), channel_id=1, replica_groups=mesh['groups'=2,'row'=128,'col'=2] {'row'}, dimensions={0} | all-to-all | bytes 524288 | tf_op jit(solution)/shard_map/all_to_all | solution.py:74
  175.7 0.2 reshape.75
  175.9 1.5 convert_reduce_fusion.1
  177.4 0.1 reshape.67
  177.5 0.1 reduce_sum.48
  177.7 0.2 multiply_reduce_fusion
  177.9 0.0 copy-start.8
  177.9 0.0 copy-start.9
  177.9 0.6 copy-done.8
  178.5 0.0 copy-done.9
  178.6 0.0 copy-start.3
  178.6 0.0 copy-start.10
  178.6 0.3 add_convert_fusion
  178.9 0.4 copy-done.3
  179.3 0.0 copy-done.10
  179.3 0.0 copy-start.11
  179.3 0.3 convolution_add_fusion.2
  179.6 0.5 copy-done.11
  180.1 0.0 copy-done.12
  180.1 1.2 fusion.7
  (8 shorter events, 0.1 us)
Async XLA Ops:
  0.0 1.6 copy-start
  0.0 1.2 copy-start.1
  1.6 0.7 copy-start.4
  1.6 0.7 copy-start.5
  1.6 0.7 copy-start.6
  2.3 0.8 copy-start.2
  2.3 0.8 copy-start.7
  177.9 0.7 copy-start.8
  177.9 0.7 copy-start.9
  178.6 0.8 copy-start.3
  178.6 0.8 copy-start.10
  179.3 0.8 copy-start.11
  179.3 0.8 copy-start.12
where the time goes:
time: 182 us; the launch traced here: 181 us
  blocking collectives  167 us (92%)
  other arithmetic  6.34 us (3%)
  local copies, waits for them, and re-layouts  4.61 us (3%)
  matrix products  2.68 us (1%)
    all_to_all x1, blocking collectives, sent_together(): lax.all_to_all(both, axis, split_axis=split_dim, concat_axis=concat_dim,...  113 us
    all_to_all x1, blocking collectives, per_device(): lax.all_to_all(triangle_chan, 'row', split_axis=1, concat_axis=0, tiled=T...  50.3 us
    all_to_all x1, blocking collectives, summed_on_arrival(): tiles = lax.all_to_all(split_up(shard, dim, length), axis, 0, 0, tiled=True)  4.59 us

commit v1 on v0

v1 whole, which is shorter than its diff:
```python
import jax
import jax.numpy as jnp
from jax import lax
from jax.experimental import pallas as pl
from jax.experimental.pallas import tpu as pltpu
from jax.sharding import PartitionSpec as P

LANES = 128


def column(row, width):
    return jnp.broadcast_to(row, (width, row.shape[1])).T


def edges_kernel(
    pair_ref, gain_ref, shift_ref, lw_ref, lb_ref, rw_ref, rb_ref, gw_ref, gb_ref,
    edge_ref, gate_ref, held_ref,
):
    rows, cols, chans = pair_ref.shape
    hidden = lw_ref.shape[1] // 2
    values = pair_ref[...].reshape(rows * cols, chans).astype(jnp.float32)
    center = values - jnp.mean(values, axis=1, keepdims=True)
    spread = jnp.mean(center * center, axis=1, keepdims=True)
    normed = (center * lax.rsqrt(spread + 1e-05) * gain_ref[...] + shift_ref[...]).astype(jnp.bfloat16)
    for side, (w_ref, b_ref) in enumerate(((lw_ref, lb_ref), (rw_ref, rb_ref))):
        gate_bias = column(b_ref[:, :hidden], LANES)[:, :1]
        value_bias = column(b_ref[:, hidden:], LANES)[:, :1]
        turned = w_ref[...].T
        for r in range(rows):
            part = normed[r * cols : (r + 1) * cols]
            joined = lax.dot_general(
                turned, part, (((1,), (1,)), ((), ())), preferred_element_type=jnp.float32
            )
            edge = jax.nn.sigmoid(joined[:hidden] + gate_bias) * (joined[hidden:] + value_bias)
            held_ref[:, r, side * cols : (side + 1) * cols] = edge
    edge_ref[...] = held_ref[...].astype(jnp.bfloat16)
    gate_ref[...] = jax.nn.sigmoid(
        jnp.dot(normed, gw_ref[...], preferred_element_type=jnp.float32) + gb_ref[...]
    )


def update_kernel(tri_ref, gate_ref, gain_ref, shift_ref, w_ref, b_ref, out_ref, held_ref):
    hidden, subs, lanes = tri_ref.shape
    values = tri_ref[...].astype(jnp.float32)
    center = values - jnp.mean(values, axis=0, keepdims=True)
    spread = jnp.mean(center * center, axis=0, keepdims=True)
    held_ref[...] = center * lax.rsqrt(spread + 1e-05)
    gain = column(gain_ref[...], lanes)
    shift = column(shift_ref[...], lanes)
    for s in range(subs):
        mixed = (held_ref[:, s, :] * gain + shift).astype(jnp.bfloat16)
        projected = lax.dot_general(
            mixed, w_ref[...], (((0,), (0,)), ((), ())), preferred_element_type=jnp.float32
        )
        at = slice(s * lanes, (s + 1) * lanes)
        out_ref[at, :] = (gate_ref[at, :] * (projected + b_ref[...])).astype(jnp.bfloat16)


def per_device(
    pair_act,
    in_gain,
    in_shift,
    left_weight,
    left_bias,
    right_weight,
    right_bias,
    gate_weight,
    gate_bias,
    out_gain,
    out_shift,
    out_weight,
    out_bias,
):
    rows, cols, chans = pair_act.shape
    hidden = left_weight.shape[1] // 2
    spots = rows * cols
    peers = lax.axis_size("row")
    halves = lax.axis_size("col")
    length = peers * rows

    def row(v):
        return v.reshape(1, -1)

    edges, gate = pl.pallas_call(
        edges_kernel,
        out_shape=(
            jax.ShapeDtypeStruct((hidden, rows, 2 * cols), jnp.bfloat16),
            jax.ShapeDtypeStruct((spots, chans), jnp.float32),
        ),
        scratch_shapes=[pltpu.VMEM((hidden, rows, 2 * cols), jnp.float32)],
    )(
        pair_act, row(in_gain), row(in_shift), left_weight, row(left_bias),
        right_weight, row(right_bias), gate_weight, row(gate_bias),
    )
    got = lax.all_to_all(edges, "row", split_axis=0, concat_axis=0, tiled=True)
    got = got.reshape(length, 2 * cols)
    left, right = got[:, :cols], got[:, cols:]
    me = lax.axis_index("col")
    half = length // halves

    def partial_sums(which):
        some = lax.dynamic_slice_in_dim(right, which * half, half, axis=0)
        return lax.dot_general(
            left, some, (((1,), (1,)), ((), ())), preferred_element_type=jnp.float32
        )

    away = lax.ppermute(partial_sums(1 - me), "col", [(0, 1), (1, 0)])
    triangle = (partial_sums(me) + away).astype(jnp.bfloat16)
    triangle = lax.all_to_all(
        triangle.reshape(peers, spots // LANES, LANES), "row", split_axis=0, concat_axis=0, tiled=True
    )
    update = pl.pallas_call(
        update_kernel,
        out_shape=jax.ShapeDtypeStruct((spots, chans), jnp.bfloat16),
        scratch_shapes=[pltpu.VMEM((hidden, spots // LANES, LANES), jnp.float32)],
    )(triangle, gate, row(out_gain), row(out_shift), out_weight, row(out_bias))
    return update.reshape(rows, cols, chans)


def solution(mesh):
    in_specs = (P(("groups", "row"), "col", None),) + (P(),) * 12
    out_specs = P(("groups", "row"), "col", None)
    return jax.shard_map(
        per_device, mesh=mesh, in_specs=in_specs, out_specs=out_specs, check_vma=False
    )
```

time: 182 us -> 174 us (0.956)
  blocking collectives: 167 us -> 50.4 us
  waiting for transfers between devices: 0 us -> 63.9 us
  starting transfers between devices: 0 us -> 52.6 us
  other arithmetic: 6.34 us -> 0 us
  Pallas kernels: 0 us -> 6.11 us
  local copies, waits for them, and re-layouts: 4.61 us -> 0.23 us
  matrix products: 2.68 us -> 0.53 us
    all_to_all x3 -> x1, blocking collectives: 167 us -> 50.4 us  [per_device(): lax.all_to_all(triangle.reshape(peers, spots // LANES, LANES), 'row', spl...]
    all_to_all x0 -> x1, waiting for transfers between devices: none -> 62.1 us  [per_device(): got = lax.all_to_all(edges, 'row', split_axis=0, concat_axis=0, tiled=True)]
    all_to_all x0 -> x1, starting transfers between devices: none -> 50.7 us  [per_device(): got = lax.all_to_all(edges, 'row', split_axis=0, concat_axis=0, tiled=True)]
    pallas_call x0 -> x2, Pallas kernels: none -> 6.11 us  [the longest x1 3.47 us: per_device(): pl.pallas_call(edges_kernel, out_shape=(jax.ShapeDtypeStruct((hidden, row...]
    unnamed x29 -> x0, local copies, waits for them, and re-layouts: 3.52 us -> none
    unnamed x1 -> x0, other arithmetic: 2.21 us -> none
    dot_general x5 -> x2, matrix products: 2.68 us -> 0.53 us  [partial_sums(): lax.dot_general(left, some, (((1,), (1,)), ((), ())), preferred_element_t...]
    convert_element_type x3 -> x0, other arithmetic: 2.1 us -> none  [the longest x1 1.48 us: per_device(): triangle.astype(jnp.float32)]
  transfers between devices with their start and end apart: 0 -> 2, of which waited for: 0 -> 2; matrix products, arithmetic and copies ran while one was open for 0% -> 0% of each run, Pallas kernels for 0% -> 0%
where the time goes in v1:
time: 174 us
  waiting for transfers between devices  63.9 us (37%)
  starting transfers between devices  52.6 us (30%)
  blocking collectives  50.4 us (29%)
  Pallas kernels  6.11 us (4%)
    all_to_all x1, waiting for transfers between devices, per_device(): got = lax.all_to_all(edges, 'row', split_axis=0, concat_axis=0, tiled=True)  62.1 us
    all_to_all x1, starting transfers between devices, per_device(): got = lax.all_to_all(edges, 'row', split_axis=0, concat_axis=0, tiled=True)  50.7 us
    all_to_all x1, blocking collectives, per_device(): lax.all_to_all(triangle.reshape(peers, spots // LANES, LANES), 'row', spl...  50.4 us
  transfers between devices with their start and end apart: 2, of which 2 were waited for; matrix products, arithmetic and copies ran while one was open for 0% of the time, Pallas kernels for 0%

profile of v1, /device:TPU:38, one launch (start us, length us, event | category | flops | bytes accessed | tf_op | source)
XLA Modules:
  0.0 173.9 jit_solution(16090982411184069999)
XLA Ops:
  0.0 3.5 %shard_map.127 = (bf16[128,4,512]{2,1,0:T(4,128)(2,1)}, f32[1024,128]{1,0:T(8,128)}) custom-call(bf16[4,256,128]{2,1,0:T(8,128)(2,1)} %pair_ref.1, f32[1,128]{1,0:T(1,128)} %bitcast.11, f32[1,128]{1,0:T(1,128)} %bitcast.12, bf16[128,256]{1,0:T(8,128)(2,1)} %lw_ref.1, f32[1,256]{1,0:T(1,128)} %bitcast.9, bf16[128,256]{1,0:T(8,128)(2,1)} %rw_ref.1, ...), custom_call_target="tpu_custom_call" | custom-call | tf_op jit(solution)/shard_map/pallas_call | solution.py:84
  3.5 50.7 %all-to-all-start = ((bf16[128,4,512]{2,1,0:T(4,128)(2,1)}), bf16[128,4,512]{2,1,0:T(4,128)(2,1)S(1)}, u32[]{:S(2)}, u32[]{:S(2)}) async-start(bf16[128,4,512]{2,1,0:T(4,128)(2,1)} %get-tuple-element.7), calls=%async_computation | async-start | bytes 1048576 | tf_op jit(solution)/shard_map/all_to_all | solution.py:95
  54.2 62.1 %all-to-all-done = bf16[128,4,512]{2,1,0:T(4,128)(2,1)S(1)} async-done(((bf16[128,4,512]{2,1,0:T(4,128)(2,1)}), bf16[128,4,512]{2,1,0:T(4,128)(2,1)S(1)}, u32[]{:S(2)}, u32[]{:S(2)}) %all-to-all-start) | async-done | bytes 524320 | tf_op jit(solution)/shard_map/all_to_all | solution.py:95
  116.2 0.1 reshape.38
  116.4 0.3 fusion.1
  116.6 2.0 %collective-permute-start = (f32[512,256]{1,0:T(8,128)S(1)}, f32[512,256]{1,0:T(8,128)S(1)}, u32[]{:S(2)}, u32[]{:S(2)}) collective-permute-start(f32[512,256]{1,0:T(8,128)S(1)} %fusion.1), channel_id=1, source_target_pairs={{0,1},{1,0},{2,3},{3,2},{4,5},{5,4},{6,7},{7,6},{8,9},{9,8},{10,11... | collective-permute-start | bytes 1572872 | tf_op jit(solution)/shard_map/ppermute | solution.py:107
  118.6 1.9 %collective-permute-done = f32[512,256]{1,0:T(8,128)S(1)} collective-permute-done((f32[512,256]{1,0:T(8,128)S(1)}, f32[512,256]{1,0:T(8,128)S(1)}, u32[]{:S(2)}, u32[]{:S(2)}) %collective-permute-start) | collective-permute-done | bytes 524320 | tf_op jit(solution)/shard_map/ppermute | solution.py:107
  120.5 0.3 fusion
  120.7 0.1 reshape.39
  120.8 50.4 %all_to_all.10.tri_ref = bf16[128,8,128]{2,1,0:T(8,128)(2,1)} all-to-all(bf16[128,8,128]{2,1,0:T(8,128)(2,1)S(1)} %reshape.39), channel_id=1, replica_groups=mesh['groups'=2,'row'=128,'col'=2] {'row'}, dimensions={0} | all-to-all | bytes 524288 | tf_op jit(solution)/shard_map/all_to_all | solution.py:109
  171.2 2.6 %shard_map.128 = bf16[1024,128]{1,0:T(8,128)(2,1)} custom-call(bf16[128,8,128]{2,1,0:T(8,128)(2,1)} %all_to_all.10.tri_ref, f32[1024,128]{1,0:T(8,128)} %get-tuple-element.8.gate_ref, f32[1,128]{1,0:T(1,128)} %bitcast.14, f32[1,128]{1,0:T(1,128)} %bitcast.15, bf16[128,128]{1,0:T(8,128)(2,1)} %w_ref.1, f32[1,128]{1,0:T(1,128)} %bitcast.16), custom_call_target="tpu_custom_call" | custom-call | tf_op jit(solution)/shard_map/pallas_call | solution.py:112
  (1 shorter events, 0.0 us)
Async XLA Ops:
  3.5 112.7 %all-to-all-start = ((bf16[128,4,512]{2,1,0:T(4,128)(2,1)}), bf16[128,4,512]{2,1,0:T(4,128)(2,1)S(1)}, u32[]{:S(2)}, u32[]{:S(2)}) async-start(bf16[128,4,512]{2,1,0:T(4,128)(2,1)} %get-tuple-element.7), calls=%async_computation | async-start | bytes 1048576 | tf_op jit(solution)/shard_map/all_to_all | solution.py:95
  116.6 3.8 %collective-permute-start = (f32[512,256]{1,0:T(8,128)S(1)}, f32[512,256]{1,0:T(8,128)S(1)}, u32[]{:S(2)}, u32[]{:S(2)}) collective-permute-start(f32[512,256]{1,0:T(8,128)S(1)} %fusion.1), channel_id=1, source_target_pairs={{0,1},{1,0},{2,3},{3,2},{4,5},{5,4},{6,7},{7,6},{8,9},{9,8},{10,11... | collective-permute-start | bytes 1572872 | tf_op jit(solution)/shard_map/ppermute | solution.py:107

commit v2 on v1

--- a/solution.py
+++ b/solution.py
@@ -6,22 +6,29 @@
 from jax.sharding import PartitionSpec as P
 
 LANES = 128
+SMALL = pltpu.CompilerParams(vmem_limit_bytes=16 * 2**20)
 
 
 def column(row, width):
     return jnp.broadcast_to(row, (width, row.shape[1])).T
 
 
-def edges_kernel(
-    pair_ref, gain_ref, shift_ref, lw_ref, lb_ref, rw_ref, rb_ref, gw_ref, gb_ref,
-    edge_ref, gate_ref, held_ref,
-):
+def edges_kernel(*refs):
+    hbm, (edge_ref, gate_ref), held_ref, vmem, sems = refs[:9], refs[9:11], refs[11], refs[12:21], refs[21]
+    loads = [pltpu.make_async_copy(h, v, sems.at[n]) for n, (h, v) in enumerate(zip(hbm, vmem))]
+    for load in loads:
+        load.start()
+    pair_ref, gain_ref, shift_ref, lw_ref, lb_ref, rw_ref, rb_ref, gw_ref, gb_ref = vmem
     rows, cols, chans = pair_ref.shape
     hidden = lw_ref.shape[1] // 2
+    for load in loads[:3]:
+        load.wait()
     values = pair_ref[...].reshape(rows * cols, chans).astype(jnp.float32)
     center = values - jnp.mean(values, axis=1, keepdims=True)
     spread = jnp.mean(center * center, axis=1, keepdims=True)
     normed = (center * lax.rsqrt(spread + 1e-05) * gain_ref[...] + shift_ref[...]).astype(jnp.bfloat16)
+    for load in loads[3:]:
+        load.wait()
     for side, (w_ref, b_ref) in enumerate(((lw_ref, lb_ref), (rw_ref, rb_ref))):
         gate_bias = column(b_ref[:, :hidden], LANES)[:, :1]
         value_bias = column(b_ref[:, hidden:], LANES)[:, :1]
@@ -81,31 +88,39 @@
     def row(v):
         return v.reshape(1, -1)
 
+    given = (
+        pair_act, row(in_gain), row(in_shift), left_weight, row(left_bias),
+        right_weight, row(right_bias), gate_weight, row(gate_bias),
+    )
     edges, gate = pl.pallas_call(
         edges_kernel,
         out_shape=(
             jax.ShapeDtypeStruct((hidden, rows, 2 * cols), jnp.bfloat16),
             jax.ShapeDtypeStruct((spots, chans), jnp.float32),
         ),
-        scratch_shapes=[pltpu.VMEM((hidden, rows, 2 * cols), jnp.float32)],
-    )(
-        pair_act, row(in_gain), row(in_shift), left_weight, row(left_bias),
-        right_weight, row(right_bias), gate_weight, row(gate_bias),
-    )
+        in_specs=[pl.BlockSpec(memory_space=pltpu.HBM)] * len(given),
+        scratch_shapes=[
+            pltpu.VMEM((hidden, rows, 2 * cols), jnp.float32),
+            *(pltpu.VMEM(v.shape, v.dtype) for v in given),
+            pltpu.SemaphoreType.DMA((len(given),)),
+        ],
+        compiler_params=SMALL,
+    )(*(pltpu.with_memory_space_constraint(v, pltpu.HBM) for v in given))
+    half = length // halves
+    me = lax.axis_index("col").astype(jnp.uint32)
+    edges, mine, other = lax.optimization_barrier((edges, me * half, (1 - me) * half))
     got = lax.all_to_all(edges, "row", split_axis=0, concat_axis=0, tiled=True)
     got = got.reshape(length, 2 * cols)
     left, right = got[:, :cols], got[:, cols:]
-    me = lax.axis_index("col")
-    half = length // halves
 
-    def partial_sums(which):
-        some = lax.dynamic_slice_in_dim(right, which * half, half, axis=0)
+    def partial_sums(start):
+        some = lax.dynamic_slice_in_dim(right, start, half, axis=0)
         return lax.dot_general(
             left, some, (((1,), (1,)), ((), ())), preferred_element_type=jnp.float32
         )
 
-    away = lax.ppermute(partial_sums(1 - me), "col", [(0, 1), (1, 0)])
-    triangle = (partial_sums(me) + away).astype(jnp.bfloat16)
+    away = lax.ppermute(partial_sums(other), "col", [(0, 1), (1, 0)])
+    triangle = (partial_sums(mine) + away).astype(jnp.bfloat16)
     triangle = lax.all_to_all(
         triangle.reshape(peers, spots // LANES, LANES), "row", split_axis=0, concat_axis=0, tiled=True
     )
@@ -113,6 +128,7 @@
         update_kernel,
         out_shape=jax.ShapeDtypeStruct((spots, chans), jnp.bfloat16),
         scratch_shapes=[pltpu.VMEM((hidden, spots // LANES, LANES), jnp.float32)],
+        compiler_params=SMALL,
     )(triangle, gate, row(out_gain), row(out_shift), out_weight, row(out_bias))
     return update.reshape(rows, cols, chans)
 

time: 174 us -> 172 us (0.989)
  blocking collectives: 50.4 us -> 163 us
  waiting for transfers between devices: 63.9 us -> 1.88 us
  starting transfers between devices: 52.6 us -> 1.95 us
  Pallas kernels: 6.11 us -> 3.93 us
    all_to_all x0 -> x1, blocking collectives: none -> 113 us  [per_device(): got = lax.all_to_all(edges, 'row', split_axis=0, concat_axis=0, tiled=True)]
    all_to_all x1 -> x0, waiting for transfers between devices: 62.1 us -> none  [per_device(): got = lax.all_to_all(edges, 'row', split_axis=0, concat_axis=0, tiled=True)]
    all_to_all x1 -> x0, starting transfers between devices: 50.7 us -> none  [per_device(): got = lax.all_to_all(edges, 'row', split_axis=0, concat_axis=0, tiled=True)]
  transfers between devices with their start and end apart: 2 -> 1, of which waited for: 2 -> 1; matrix products, arithmetic and copies ran while one was open for 0% -> 0% of each run, Pallas kernels for 0% -> 0%
where the time goes in v2:
time: 172 us
  blocking collectives  163 us (95%)
  Pallas kernels  3.93 us (2%)
  starting transfers between devices  1.95 us (1%)
  waiting for transfers between devices  1.88 us (1%)
    all_to_all x1, blocking collectives, per_device(): got = lax.all_to_all(edges, 'row', split_axis=0, concat_axis=0, tiled=True)  113 us
    all_to_all x1, blocking collectives, per_device(): lax.all_to_all(triangle.reshape(peers, spots // LANES, LANES), 'row', spl...  50.3 us
  transfers between devices with their start and end apart: 1, of which 1 were waited for; matrix products, arithmetic and copies ran while one was open for 0% of the time, Pallas kernels for 0%

profile of v2, /device:TPU:38, one launch (start us, length us, event | category | flops | bytes accessed | tf_op | source)
XLA Modules:
  0.0 172.1 jit_solution(2586039311049114610)
XLA Ops:
  0.0 2.4 %shard_map.127 = (bf16[128,4,512]{2,1,0:T(4,128)(2,1)S(1)}, f32[1024,128]{1,0:T(8,128)S(1)}) custom-call(bf16[4,256,128]{2,1,0:T(8,128)(2,1)} %refs_0_.1, f32[1,128]{1,0:T(1,128)} %bitcast.14, f32[1,128]{1,0:T(1,128)} %bitcast.15, bf16[128,256]{1,0:T(8,128)(2,1)} %refs_3_.1, f32[1,256]{1,0:T(1,128)} %bitcast.12, bf16[128,256]{1,0:T(8,128)(2,1)} %refs_5_.1, ...), custom_call_target="tpu_custom_call" | custom-call | tf_op jit(solution)/shard_map/pallas_call | solution.py:95
  2.4 112.5 %all_to_all.10 = bf16[128,4,512]{2,1,0:T(4,128)(2,1)S(1)} all-to-all(bf16[128,4,512]{2,1,0:T(4,128)(2,1)S(1)} %get-tuple-element.11), channel_id=1, replica_groups=mesh['groups'=2,'row'=128,'col'=2] {'row'}, dimensions={0} | all-to-all | bytes 1048576 | tf_op jit(solution)/shard_map/all_to_all | solution.py:112
  115.0 0.1 reshape.38
  115.1 0.3 fusion.1
  115.4 2.0 %collective-permute-start = (f32[512,256]{1,0:T(8,128)S(1)}, f32[512,256]{1,0:T(8,128)S(1)}, u32[]{:S(2)}, u32[]{:S(2)}) collective-permute-start(f32[512,256]{1,0:T(8,128)S(1)} %fusion.1), channel_id=1, source_target_pairs={{0,1},{1,0},{2,3},{3,2},{4,5},{5,4},{6,7},{7,6},{8,9},{9,8},{10,11... | collective-permute-start | bytes 1572872 | tf_op jit(solution)/shard_map/ppermute | solution.py:122
  117.3 1.9 %collective-permute-done = f32[512,256]{1,0:T(8,128)S(1)} collective-permute-done((f32[512,256]{1,0:T(8,128)S(1)}, f32[512,256]{1,0:T(8,128)S(1)}, u32[]{:S(2)}, u32[]{:S(2)}) %collective-permute-start) | collective-permute-done | bytes 524320 | tf_op jit(solution)/shard_map/ppermute | solution.py:122
  119.2 0.3 fusion
  119.5 0.1 reshape.39
  119.6 0.0 copy-start
  119.6 50.3 %all_to_all.11.tri_ref = bf16[128,8,128]{2,1,0:T(8,128)(2,1)S(1)} all-to-all(bf16[128,8,128]{2,1,0:T(8,128)(2,1)S(1)} %reshape.39), channel_id=1, replica_groups=mesh['groups'=2,'row'=128,'col'=2] {'row'}, dimensions={0} | all-to-all | bytes 524288 | tf_op jit(solution)/shard_map/all_to_all | solution.py:124
  169.9 0.0 copy-start.1
  169.9 0.0 copy-start.2
  169.9 0.0 copy-start.3
  169.9 0.0 copy-done
  169.9 0.6 copy-done.1
  170.6 0.0 copy-done.2
  170.6 0.0 copy-done.3
  170.6 1.5 shard_map.128
  (1 shorter events, 0.0 us)
Async XLA Ops:
  115.4 3.8 %collective-permute-start = (f32[512,256]{1,0:T(8,128)S(1)}, f32[512,256]{1,0:T(8,128)S(1)}, u32[]{:S(2)}, u32[]{:S(2)}) collective-permute-start(f32[512,256]{1,0:T(8,128)S(1)} %fusion.1), channel_id=1, source_target_pairs={{0,1},{1,0},{2,3},{3,2},{4,5},{5,4},{6,7},{7,6},{8,9},{9,8},{10,11... | collective-permute-start | bytes 1572872 | tf_op jit(solution)/shard_map/ppermute | solution.py:122
  119.6 50.3 %copy-start = (bf16[128,128]{1,0:T(8,128)(2,1)S(1)}, bf16[128,128]{1,0:T(8,128)(2,1)}, u32[]{:S(2)}) copy-start(bf16[128,128]{1,0:T(8,128)(2,1)} %w_ref.1) | copy-start | bytes 98308
  169.9 0.7 copy-start.1
  169.9 0.7 copy-start.2
  169.9 0.7 copy-start.3

commit v3 on v2

--- a/solution.py
+++ b/solution.py
@@ -14,8 +14,9 @@
 
 
 def edges_kernel(*refs):
-    hbm, (edge_ref, gate_ref), held_ref, vmem, sems = refs[:9], refs[9:11], refs[11], refs[12:21], refs[21]
-    loads = [pltpu.make_async_copy(h, v, sems.at[n]) for n, (h, v) in enumerate(zip(hbm, vmem))]
+    hbm, edge_ref, gate_ref, kept, held_ref = refs[:13], refs[13], refs[14], refs[15:19], refs[19]
+    vmem, sems = refs[20:29], refs[29]
+    loads = [pltpu.make_async_copy(h, v, sems.at[n]) for n, (h, v) in enumerate(zip(hbm, vmem + kept))]
     for load in loads:
         load.start()
     pair_ref, gain_ref, shift_ref, lw_ref, lb_ref, rw_ref, rb_ref, gw_ref, gb_ref = vmem
@@ -92,24 +93,27 @@
         pair_act, row(in_gain), row(in_shift), left_weight, row(left_bias),
         right_weight, row(right_bias), gate_weight, row(gate_bias),
     )
-    edges, gate = pl.pallas_call(
+    closing = (row(out_gain), row(out_shift), out_weight, row(out_bias))
+    edges, gate, *closing = pl.pallas_call(
         edges_kernel,
         out_shape=(
             jax.ShapeDtypeStruct((hidden, rows, 2 * cols), jnp.bfloat16),
             jax.ShapeDtypeStruct((spots, chans), jnp.float32),
+            *(jax.ShapeDtypeStruct(v.shape, v.dtype) for v in closing),
         ),
-        in_specs=[pl.BlockSpec(memory_space=pltpu.HBM)] * len(given),
+        in_specs=[pl.BlockSpec(memory_space=pltpu.HBM)] * (len(given) + len(closing)),
         scratch_shapes=[
             pltpu.VMEM((hidden, rows, 2 * cols), jnp.float32),
             *(pltpu.VMEM(v.shape, v.dtype) for v in given),
-            pltpu.SemaphoreType.DMA((len(given),)),
+            pltpu.SemaphoreType.DMA((len(given) + len(closing),)),
         ],
         compiler_params=SMALL,
-    )(*(pltpu.with_memory_space_constraint(v, pltpu.HBM) for v in given))
+    )(*(pltpu.with_memory_space_constraint(v, pltpu.HBM) for v in (*given, *closing)))
     half = length // halves
     me = lax.axis_index("col").astype(jnp.uint32)
-    edges, mine, other = lax.optimization_barrier((edges, me * half, (1 - me) * half))
-    got = lax.all_to_all(edges, "row", split_axis=0, concat_axis=0, tiled=True)
+    order = [(peers // 2 + n) % peers for n in range(peers)]
+    edges, mine, other = lax.optimization_barrier((edges, (1 - me) * half, me * half))
+    got = lax.all_to_all(edges, "row", split_axis=0, concat_axis=0, axis_index_groups=[order], tiled=True)
     got = got.reshape(length, 2 * cols)
     left, right = got[:, :cols], got[:, cols:]
 
@@ -122,14 +126,14 @@
     away = lax.ppermute(partial_sums(other), "col", [(0, 1), (1, 0)])
     triangle = (partial_sums(mine) + away).astype(jnp.bfloat16)
     triangle = lax.all_to_all(
-        triangle.reshape(peers, spots // LANES, LANES), "row", split_axis=0, concat_axis=0, tiled=True
+        triangle.reshape(peers, spots // LANES, LANES), "row", split_axis=0, concat_axis=0, axis_index_groups=[order], tiled=True
     )
     update = pl.pallas_call(
         update_kernel,
         out_shape=jax.ShapeDtypeStruct((spots, chans), jnp.bfloat16),
         scratch_shapes=[pltpu.VMEM((hidden, spots // LANES, LANES), jnp.float32)],
         compiler_params=SMALL,
-    )(triangle, gate, row(out_gain), row(out_shift), out_weight, row(out_bias))
+    )(triangle, gate, *closing)
     return update.reshape(rows, cols, chans)
 
 

time: 172 us -> 173 us (level); the launches traced: 172 us -> 170 us
  blocking collectives: 163 us -> 161 us
where the time goes in v3:
time: 173 us; the launch traced here: 170 us
  blocking collectives  161 us (93%)
  Pallas kernels  3.98 us (2%)
  starting transfers between devices  1.95 us (1%)
  waiting for transfers between devices  1.88 us (1%)
    all_to_all x1, blocking collectives, per_device(): lax.all_to_all(edges, 'row', split_axis=0, concat_axis=0, axis_index_grou...  111 us
    all_to_all x1, blocking collectives, per_device(): lax.all_to_all(triangle.reshape(peers, spots // LANES, LANES), 'row', spl...  50 us
  transfers between devices with their start and end apart: 1, of which 1 were waited for; matrix products, arithmetic and copies ran while one was open for 0% of the time, Pallas kernels for 0%

profile of v3, /device:TPU:38, one launch (start us, length us, event | category | flops | bytes accessed | tf_op | source)
XLA Modules:
  0.0 170.0 jit_solution(5529011128439455582)
XLA Ops:
  0.0 2.5 %shard_map.127 = (bf16[128,4,512]{2,1,0:T(4,128)(2,1)S(1)}, f32[1024,128]{1,0:T(8,128)S(1)}, f32[1,128]{1,0:T(1,128)S(1)}, f32[1,128]{1,0:T(1,128)S(1)}, bf16[12...) custom-call(bf16[4,256,128]{2,1,0:T(8,128)(2,1)} %refs_0_.1, f32[1,128]{1,0:T(1,128)} %bitcast.11, f32[1,128]{1,0:T(1,128)} %bitcast.12, ...), custom_call_target="tpu_custom_call" | custom-call | tf_op jit(solution)/shard_map/pallas_call | solution.py:97
  2.5 111.4 %all_to_all.10 = bf16[128,4,512]{2,1,0:T(4,128)(2,1)S(1)} all-to-all(bf16[128,4,512]{2,1,0:T(4,128)(2,1)S(1)} %get-tuple-element.15), channel_id=1, replica_groups={{128,130,132,134,136,138,140,142,144,146,148,150,152,154,156,158,160,16..., dimensions={0} | all-to-all | bytes 1048576 | tf_op jit(solution)/shard_map/all_to_all | solution.py:116
  113.9 0.1 reshape.41
  114.0 0.3 fusion.1
  114.3 2.0 %collective-permute-start = (f32[512,256]{1,0:T(8,128)S(1)}, f32[512,256]{1,0:T(8,128)S(1)}, u32[]{:S(2)}, u32[]{:S(2)}) collective-permute-start(f32[512,256]{1,0:T(8,128)S(1)} %fusion.1), channel_id=1, source_target_pairs={{0,1},{1,0},{2,3},{3,2},{4,5},{5,4},{6,7},{7,6},{8,9},{9,8},{10,11... | collective-permute-start | bytes 1572872 | tf_op jit(solution)/shard_map/ppermute | solution.py:126
  116.3 1.9 %collective-permute-done = f32[512,256]{1,0:T(8,128)S(1)} collective-permute-done((f32[512,256]{1,0:T(8,128)S(1)}, f32[512,256]{1,0:T(8,128)S(1)}, u32[]{:S(2)}, u32[]{:S(2)}) %collective-permute-start) | collective-permute-done | bytes 524320 | tf_op jit(solution)/shard_map/ppermute | solution.py:126
  118.1 0.3 fusion
  118.4 0.1 reshape.42
  118.5 50.0 %all_to_all.11.tri_ref = bf16[128,8,128]{2,1,0:T(8,128)(2,1)S(1)} all-to-all(bf16[128,8,128]{2,1,0:T(8,128)(2,1)S(1)} %reshape.42), channel_id=1, replica_groups={{128,130,132,134,136,138,140,142,144,146,148,150,152,154,156,158,160,16..., dimensions={0} | all-to-all | bytes 524288 | tf_op jit(solution)/shard_map/all_to_all | solution.py:128
  168.5 1.5 shard_map.128
  (1 shorter events, 0.0 us)
Async XLA Ops:
  114.3 3.8 %collective-permute-start = (f32[512,256]{1,0:T(8,128)S(1)}, f32[512,256]{1,0:T(8,128)S(1)}, u32[]{:S(2)}, u32[]{:S(2)}) collective-permute-start(f32[512,256]{1,0:T(8,128)S(1)} %fusion.1), channel_id=1, source_target_pairs={{0,1},{1,0},{2,3},{3,2},{4,5},{5,4},{6,7},{7,6},{8,9},{9,8},{10,11... | collective-permute-start | bytes 1572872 | tf_op jit(solution)/shard_map/ppermute | solution.py:126

commit v4 on v3

--- a/solution.py
+++ b/solution.py
@@ -40,7 +40,9 @@
                 turned, part, (((1,), (1,)), ((), ())), preferred_element_type=jnp.float32
             )
             edge = jax.nn.sigmoid(joined[:hidden] + gate_bias) * (joined[hidden:] + value_bias)
-            held_ref[:, r, side * cols : (side + 1) * cols] = edge
+            at = slice(side * cols, (side + 1) * cols)
+            held_ref[: hidden // 2, r, at] = edge[hidden // 2 :]
+            held_ref[hidden // 2 :, r, at] = edge[: hidden // 2]
     edge_ref[...] = held_ref[...].astype(jnp.bfloat16)
     gate_ref[...] = jax.nn.sigmoid(
         jnp.dot(normed, gw_ref[...], preferred_element_type=jnp.float32) + gb_ref[...]
@@ -112,10 +114,12 @@
     half = length // halves
     me = lax.axis_index("col").astype(jnp.uint32)
     order = [(peers // 2 + n) % peers for n in range(peers)]
-    edges, mine, other = lax.optimization_barrier((edges, (1 - me) * half, me * half))
-    got = lax.all_to_all(edges, "row", split_axis=0, concat_axis=0, axis_index_groups=[order], tiled=True)
+    edges, mine, other = lax.optimization_barrier((edges, me * half, (1 - me) * half))
+    got = lax.all_to_all(edges, "row", split_axis=0, concat_axis=0, tiled=True)
     got = got.reshape(length, 2 * cols)
-    left, right = got[:, :cols], got[:, cols:]
+    middle = length // 2
+    left = jnp.concatenate((got[middle:, :cols], got[:middle, :cols]))
+    right = got[:, cols:]
 
     def partial_sums(start):
         some = lax.dynamic_slice_in_dim(right, start, half, axis=0)

time: 173 us -> 173 us (level)
  no operation moved by 1% of the time
where the time goes in v4:
time: 173 us; the launch traced here: 170 us
  blocking collectives  162 us (94%)
  Pallas kernels  3.98 us (2%)
  starting transfers between devices  1.95 us (1%)
  waiting for transfers between devices  1.88 us (1%)
    all_to_all x1, blocking collectives, per_device(): got = lax.all_to_all(edges, 'row', split_axis=0, concat_axis=0, tiled=True)  113 us
    all_to_all x1, blocking collectives, per_device(): lax.all_to_all(triangle.reshape(peers, spots // LANES, LANES), 'row', spl...  49.1 us
  transfers between devices with their start and end apart: 1, of which 1 were waited for; matrix products, arithmetic and copies ran while one was open for 0% of the time, Pallas kernels for 0%

profile of v4, /device:TPU:38, one launch (start us, length us, event | category | flops | bytes accessed | tf_op | source)
XLA Modules:
  0.0 170.3 jit_solution(5972588624106122253)
XLA Ops:
  0.0 2.5 %shard_map.127 = (bf16[128,4,512]{2,1,0:T(4,128)(2,1)S(1)}, f32[1024,128]{1,0:T(8,128)S(1)}, f32[1,128]{1,0:T(1,128)S(1)}, f32[1,128]{1,0:T(1,128)S(1)}, bf16[12...) custom-call(bf16[4,256,128]{2,1,0:T(8,128)(2,1)} %refs_0_.1, f32[1,128]{1,0:T(1,128)} %bitcast.11, f32[1,128]{1,0:T(1,128)} %bitcast.12, ...), custom_call_target="tpu_custom_call" | custom-call | tf_op jit(solution)/shard_map/pallas_call | solution.py:99
  2.5 112.5 %all_to_all.10 = bf16[128,4,512]{2,1,0:T(4,128)(2,1)S(1)} all-to-all(bf16[128,4,512]{2,1,0:T(4,128)(2,1)S(1)} %get-tuple-element.15), channel_id=1, replica_groups=mesh['groups'=2,'row'=128,'col'=2] {'row'}, dimensions={0} | all-to-all | bytes 1048576 | tf_op jit(solution)/shard_map/all_to_all | solution.py:118
  115.0 0.1 reshape.41
  115.2 0.3 fusion.1
  115.5 2.0 %collective-permute-start = (f32[512,256]{1,0:T(8,128)S(1)}, f32[512,256]{1,0:T(8,128)S(1)}, u32[]{:S(2)}, u32[]{:S(2)}) collective-permute-start(f32[512,256]{1,0:T(8,128)S(1)} %fusion.1), channel_id=1, source_target_pairs={{0,1},{1,0},{2,3},{3,2},{4,5},{5,4},{6,7},{7,6},{8,9},{9,8},{10,11... | collective-permute-start | bytes 1572872 | tf_op jit(solution)/shard_map/ppermute | solution.py:130
  117.4 1.9 %collective-permute-done = f32[512,256]{1,0:T(8,128)S(1)} collective-permute-done((f32[512,256]{1,0:T(8,128)S(1)}, f32[512,256]{1,0:T(8,128)S(1)}, u32[]{:S(2)}, u32[]{:S(2)}) %collective-permute-start) | collective-permute-done | bytes 524320 | tf_op jit(solution)/shard_map/ppermute | solution.py:130
  119.3 0.3 fusion
  119.6 0.1 reshape.42
  119.7 49.1 %all_to_all.11.tri_ref = bf16[128,8,128]{2,1,0:T(8,128)(2,1)S(1)} all-to-all(bf16[128,8,128]{2,1,0:T(8,128)(2,1)S(1)} %reshape.42), channel_id=1, replica_groups={{128,130,132,134,136,138,140,142,144,146,148,150,152,154,156,158,160,16..., dimensions={0} | all-to-all | bytes 524288 | tf_op jit(solution)/shard_map/all_to_all | solution.py:132
  168.8 1.5 shard_map.128
  (2 shorter events, 0.0 us)
Async XLA Ops:
  115.5 3.8 %collective-permute-start = (f32[512,256]{1,0:T(8,128)S(1)}, f32[512,256]{1,0:T(8,128)S(1)}, u32[]{:S(2)}, u32[]{:S(2)}) collective-permute-start(f32[512,256]{1,0:T(8,128)S(1)} %fusion.1), channel_id=1, source_target_pairs={{0,1},{1,0},{2,3},{3,2},{4,5},{5,4},{6,7},{7,6},{8,9},{9,8},{10,11... | collective-permute-start | bytes 1572872 | tf_op jit(solution)/shard_map/ppermute | solution.py:130

commit v5 on v3

--- a/solution.py
+++ b/solution.py
@@ -47,7 +47,7 @@
     )
 
 
-def update_kernel(tri_ref, gate_ref, gain_ref, shift_ref, w_ref, b_ref, out_ref, held_ref):
+def update_kernel(tri_ref, gate_ref, gain_ref, shift_ref, w_ref, b_ref, out_ref, held_ref, made_ref, sems):
     hidden, subs, lanes = tri_ref.shape
     values = tri_ref[...].astype(jnp.float32)
     center = values - jnp.mean(values, axis=0, keepdims=True)
@@ -55,13 +55,18 @@
     held_ref[...] = center * lax.rsqrt(spread + 1e-05)
     gain = column(gain_ref[...], lanes)
     shift = column(shift_ref[...], lanes)
+    stores = []
     for s in range(subs):
         mixed = (held_ref[:, s, :] * gain + shift).astype(jnp.bfloat16)
         projected = lax.dot_general(
             mixed, w_ref[...], (((0,), (0,)), ((), ())), preferred_element_type=jnp.float32
         )
         at = slice(s * lanes, (s + 1) * lanes)
-        out_ref[at, :] = (gate_ref[at, :] * (projected + b_ref[...])).astype(jnp.bfloat16)
+        made_ref[at, :] = (gate_ref[at, :] * (projected + b_ref[...])).astype(jnp.bfloat16)
+        stores.append(pltpu.make_async_copy(made_ref.at[at, :], out_ref.at[at, :], sems.at[s]))
+        stores[-1].start()
+    for store in stores:
+        store.wait()
 
 
 def per_device(
@@ -111,9 +116,8 @@
     )(*(pltpu.with_memory_space_constraint(v, pltpu.HBM) for v in (*given, *closing)))
     half = length // halves
     me = lax.axis_index("col").astype(jnp.uint32)
-    order = [(peers // 2 + n) % peers for n in range(peers)]
-    edges, mine, other = lax.optimization_barrier((edges, (1 - me) * half, me * half))
-    got = lax.all_to_all(edges, "row", split_axis=0, concat_axis=0, axis_index_groups=[order], tiled=True)
+    edges, mine, other = lax.optimization_barrier((edges, me * half, (1 - me) * half))
+    got = lax.all_to_all(edges, "row", split_axis=0, concat_axis=0, tiled=True)
     got = got.reshape(length, 2 * cols)
     left, right = got[:, :cols], got[:, cols:]
 
@@ -123,15 +127,20 @@
             left, some, (((1,), (1,)), ((), ())), preferred_element_type=jnp.float32
         )
 
-    away = lax.ppermute(partial_sums(other), "col", [(0, 1), (1, 0)])
-    triangle = (partial_sums(mine) + away).astype(jnp.bfloat16)
+    away = lax.ppermute(partial_sums(other).astype(jnp.bfloat16), "col", [(0, 1), (1, 0)])
+    triangle = (partial_sums(mine) + away.astype(jnp.float32)).astype(jnp.bfloat16)
     triangle = lax.all_to_all(
-        triangle.reshape(peers, spots // LANES, LANES), "row", split_axis=0, concat_axis=0, axis_index_groups=[order], tiled=True
+        triangle.reshape(peers, spots // LANES, LANES), "row", split_axis=0, concat_axis=0, tiled=True
     )
     update = pl.pallas_call(
         update_kernel,
         out_shape=jax.ShapeDtypeStruct((spots, chans), jnp.bfloat16),
-        scratch_shapes=[pltpu.VMEM((hidden, spots // LANES, LANES), jnp.float32)],
+        out_specs=pl.BlockSpec(memory_space=pltpu.HBM),
+        scratch_shapes=[
+            pltpu.VMEM((hidden, spots // LANES, LANES), jnp.float32),
+            pltpu.VMEM((spots, chans), jnp.bfloat16),
+            pltpu.SemaphoreType.DMA((spots // LANES,)),
+        ],
         compiler_params=SMALL,
     )(triangle, gate, *closing)
     return update.reshape(rows, cols, chans)

time: 173 us -> 171 us (0.988); the launches traced: 170 us -> 171 us
  blocking collectives: 161 us -> 163 us
where the time goes in v5:
time: 171 us
  blocking collectives  163 us (95%)
  Pallas kernels  3.97 us (2%)
  starting transfers between devices  1.95 us (1%)
    all_to_all x1, blocking collectives, per_device(): got = lax.all_to_all(edges, 'row', split_axis=0, concat_axis=0, tiled=True)  113 us
    all_to_all x1, blocking collectives, per_device(): lax.all_to_all(triangle.reshape(peers, spots // LANES, LANES), 'row', spl...  50.3 us
  transfers between devices with their start and end apart: 1, of which 1 were waited for; matrix products, arithmetic and copies ran while one was open for 0% of the time, Pallas kernels for 0%

profile of v5, /device:TPU:38, one launch (start us, length us, event | category | flops | bytes accessed | tf_op | source)
XLA Modules:
  0.0 171.0 jit_solution(17312503271029506263)
XLA Ops:
  0.0 2.5 %shard_map.127 = (bf16[128,4,512]{2,1,0:T(4,128)(2,1)S(1)}, f32[1024,128]{1,0:T(8,128)S(1)}, f32[1,128]{1,0:T(1,128)S(1)}, f32[1,128]{1,0:T(1,128)S(1)}, bf16[12...) custom-call(bf16[4,256,128]{2,1,0:T(8,128)(2,1)} %refs_0_.1, f32[1,128]{1,0:T(1,128)} %bitcast.11, f32[1,128]{1,0:T(1,128)} %bitcast.12, ...), custom_call_target="tpu_custom_call" | custom-call | tf_op jit(solution)/shard_map/pallas_call | solution.py:102
  2.5 112.5 %all_to_all.10 = bf16[128,4,512]{2,1,0:T(4,128)(2,1)S(1)} all-to-all(bf16[128,4,512]{2,1,0:T(4,128)(2,1)S(1)} %get-tuple-element.15), channel_id=1, replica_groups=mesh['groups'=2,'row'=128,'col'=2] {'row'}, dimensions={0} | all-to-all | bytes 1048576 | tf_op jit(solution)/shard_map/all_to_all | solution.py:120
  115.0 0.1 reshape.41
  115.2 0.3 convolution_convert_fusion
  115.4 2.0 %collective-permute-start = (bf16[512,256]{1,0:T(8,128)(2,1)S(1)}, bf16[512,256]{1,0:T(8,128)(2,1)S(1)}, u32[]{:S(2)}, u32[]{:S(2)}) collective-permute-start(bf16[512,256]{1,0:T(8,128)(2,1)S(1)} %convolution_convert_fusion), channel_id=1, source_target_pairs={{0,1},{1,0},{2,3},{3,2},{4,5},{5,4},{6,7},{7,6},{8,9},{9,8},{10,11... | collective-permute-start | bytes 786440 | tf_op jit(solution)/shard_map/ppermute | solution.py:130
  117.4 1.5 collective-permute-done
  118.9 0.3 add_convert_fusion
  119.2 0.1 reshape.42
  119.3 50.3 %all_to_all.11.tri_ref = bf16[128,8,128]{2,1,0:T(8,128)(2,1)S(1)} all-to-all(bf16[128,8,128]{2,1,0:T(8,128)(2,1)S(1)} %reshape.42), channel_id=1, replica_groups=mesh['groups'=2,'row'=128,'col'=2] {'row'}, dimensions={0} | all-to-all | bytes 524288 | tf_op jit(solution)/shard_map/all_to_all | solution.py:132
  169.5 1.5 shard_map.128
  (1 shorter events, 0.0 us)
Async XLA Ops:
  115.4 3.5 %collective-permute-start = (bf16[512,256]{1,0:T(8,128)(2,1)S(1)}, bf16[512,256]{1,0:T(8,128)(2,1)S(1)}, u32[]{:S(2)}, u32[]{:S(2)}) collective-permute-start(bf16[512,256]{1,0:T(8,128)(2,1)S(1)} %convolution_convert_fusion), channel_id=1, source_target_pairs={{0,1},{1,0},{2,3},{3,2},{4,5},{5,4},{6,7},{7,6},{8,9},{9,8},{10,11... | collective-permute-start | bytes 786440 | tf_op jit(solution)/shard_map/ppermute | solution.py:130

commit v6 on v5

--- a/solution.py
+++ b/solution.py
@@ -40,8 +40,11 @@
                 turned, part, (((1,), (1,)), ((), ())), preferred_element_type=jnp.float32
             )
             edge = jax.nn.sigmoid(joined[:hidden] + gate_bias) * (joined[hidden:] + value_bias)
-            held_ref[:, r, side * cols : (side + 1) * cols] = edge
-    edge_ref[...] = held_ref[...].astype(jnp.bfloat16)
+            for at in range(0, cols, LANES):
+                block = (side * cols + at) // LANES
+                held_ref[block, pl.ds(r, hidden, stride=rows), :] = edge[:, at : at + LANES]
+    for block in range(held_ref.shape[0]):
+        edge_ref[:, block * LANES : (block + 1) * LANES] = held_ref[block].astype(jnp.bfloat16)
     gate_ref[...] = jax.nn.sigmoid(
         jnp.dot(normed, gw_ref[...], preferred_element_type=jnp.float32) + gb_ref[...]
     )
@@ -52,12 +55,12 @@
     values = tri_ref[...].astype(jnp.float32)
     center = values - jnp.mean(values, axis=0, keepdims=True)
     spread = jnp.mean(center * center, axis=0, keepdims=True)
-    held_ref[...] = center * lax.rsqrt(spread + 1e-05)
+    held_ref[...] = (center * lax.rsqrt(spread + 1e-05)).reshape(hidden * subs, lanes)
     gain = column(gain_ref[...], lanes)
     shift = column(shift_ref[...], lanes)
     stores = []
     for s in range(subs):
-        mixed = (held_ref[:, s, :] * gain + shift).astype(jnp.bfloat16)
+        mixed = (held_ref[pl.ds(s, hidden, stride=subs), :] * gain + shift).astype(jnp.bfloat16)
         projected = lax.dot_general(
             mixed, w_ref[...], (((0,), (0,)), ((), ())), preferred_element_type=jnp.float32
         )
@@ -102,18 +105,19 @@
     edges, gate, *closing = pl.pallas_call(
         edges_kernel,
         out_shape=(
-            jax.ShapeDtypeStruct((hidden, rows, 2 * cols), jnp.bfloat16),
+            jax.ShapeDtypeStruct((hidden * rows, 2 * cols), jnp.bfloat16),
             jax.ShapeDtypeStruct((spots, chans), jnp.float32),
             *(jax.ShapeDtypeStruct(v.shape, v.dtype) for v in closing),
         ),
         in_specs=[pl.BlockSpec(memory_space=pltpu.HBM)] * (len(given) + len(closing)),
         scratch_shapes=[
-            pltpu.VMEM((hidden, rows, 2 * cols), jnp.float32),
+            pltpu.VMEM((2 * cols // LANES, hidden * rows, LANES), jnp.float32),
             *(pltpu.VMEM(v.shape, v.dtype) for v in given),
             pltpu.SemaphoreType.DMA((len(given) + len(closing),)),
         ],
         compiler_params=SMALL,
     )(*(pltpu.with_memory_space_constraint(v, pltpu.HBM) for v in (*given, *closing)))
+    edges = edges.reshape(hidden, rows, 2 * cols)
     half = length // halves
     me = lax.axis_index("col").astype(jnp.uint32)
     edges, mine, other = lax.optimization_barrier((edges, me * half, (1 - me) * half))
@@ -137,7 +141,7 @@
         out_shape=jax.ShapeDtypeStruct((spots, chans), jnp.bfloat16),
         out_specs=pl.BlockSpec(memory_space=pltpu.HBM),
         scratch_shapes=[
-            pltpu.VMEM((hidden, spots // LANES, LANES), jnp.float32),
+            pltpu.VMEM((hidden * spots // LANES, LANES), jnp.float32),
             pltpu.VMEM((spots, chans), jnp.bfloat16),
             pltpu.SemaphoreType.DMA((spots // LANES,)),
         ],

time: 171 us -> 171 us (level)
  no operation moved by 1% of the time
where the time goes in v6:
time: 171 us
  blocking collectives  163 us (95%)
  Pallas kernels  3.37 us (2%)
  starting transfers between devices  1.95 us (1%)
    all_to_all x1, blocking collectives, per_device(): got = lax.all_to_all(edges, 'row', split_axis=0, concat_axis=0, tiled=True)  113 us
    all_to_all x1, blocking collectives, per_device(): lax.all_to_all(triangle.reshape(peers, spots // LANES, LANES), 'row', spl...  50.3 us
  transfers between devices with their start and end apart: 1, of which 1 were waited for; matrix products, arithmetic and copies ran while one was open for 0% of the time, Pallas kernels for 0%

profile of v6, /device:TPU:38, one launch (start us, length us, event | category | flops | bytes accessed | tf_op | source)
XLA Modules:
  0.0 170.6 jit_solution(11564557926812407633)
XLA Ops:
  0.0 2.1 %shard_map.127 = (bf16[512,512]{1,0:T(8,128)(2,1)S(1)}, f32[1024,128]{1,0:T(8,128)S(1)}, f32[1,128]{1,0:T(1,128)S(1)}, f32[1,128]{1,0:T(1,128)S(1)}, bf16[128,128]{1,0:T(8,128)(2,1)S(1)}, /*index=5*/f32[1,128]{1,0:T(1,128)S(1)}) custom-call(bf16[4,256,128]{2,1,0:T(8,128)(2,1)} %refs_0_.1, f32[1,128]{1,0:T(1,128)} %bitcast.11, f32[1,128]{1,0:T(1,128)} %bitcast.12, ...), custom_call_target="tpu_custom_call" | custom-call | tf_op jit(solution)/shard_map/pallas_call | solution.py:105
  2.1 0.1 reshape.44
  2.2 112.5 %all_to_all.10 = bf16[128,4,512]{2,1,0:T(4,128)(2,1)S(1)} all-to-all(bf16[128,4,512]{2,1,0:T(4,128)(2,1)S(1)} %reshape.44), channel_id=1, replica_groups=mesh['groups'=2,'row'=128,'col'=2] {'row'}, dimensions={0} | all-to-all | bytes 1048576 | tf_op jit(solution)/shard_map/all_to_all | solution.py:124
  114.7 0.1 reshape.45
  114.9 0.3 convolution_convert_fusion
  115.2 2.0 %collective-permute-start = (bf16[512,256]{1,0:T(8,128)(2,1)S(1)}, bf16[512,256]{1,0:T(8,128)(2,1)S(1)}, u32[]{:S(2)}, u32[]{:S(2)}) collective-permute-start(bf16[512,256]{1,0:T(8,128)(2,1)S(1)} %convolution_convert_fusion), channel_id=1, source_target_pairs={{0,1},{1,0},{2,3},{3,2},{4,5},{5,4},{6,7},{7,6},{8,9},{9,8},{10,11... | collective-permute-start | bytes 786440 | tf_op jit(solution)/shard_map/ppermute | solution.py:134
  117.1 1.5 collective-permute-done
  118.6 0.3 add_convert_fusion
  118.9 0.1 reshape.46
  119.0 50.3 %all_to_all.11.tri_ref = bf16[128,8,128]{2,1,0:T(8,128)(2,1)S(1)} all-to-all(bf16[128,8,128]{2,1,0:T(8,128)(2,1)S(1)} %reshape.46), channel_id=1, replica_groups=mesh['groups'=2,'row'=128,'col'=2] {'row'}, dimensions={0} | all-to-all | bytes 524288 | tf_op jit(solution)/shard_map/all_to_all | solution.py:136
  169.3 1.3 shard_map.128
  (1 shorter events, 0.0 us)
Async XLA Ops:
  115.2 3.5 %collective-permute-start = (bf16[512,256]{1,0:T(8,128)(2,1)S(1)}, bf16[512,256]{1,0:T(8,128)(2,1)S(1)}, u32[]{:S(2)}, u32[]{:S(2)}) collective-permute-start(bf16[512,256]{1,0:T(8,128)(2,1)S(1)} %convolution_convert_fusion), channel_id=1, source_target_pairs={{0,1},{1,0},{2,3},{3,2},{4,5},{5,4},{6,7},{7,6},{8,9},{9,8},{10,11... | collective-permute-start | bytes 786440 | tf_op jit(solution)/shard_map/ppermute | solution.py:134

commit v7 on v6

--- a/solution.py
+++ b/solution.py
@@ -9,8 +9,9 @@
 SMALL = pltpu.CompilerParams(vmem_limit_bytes=16 * 2**20)
 
 
-def column(row, width):
-    return jnp.broadcast_to(row, (width, row.shape[1])).T
+def columns(*rows):
+    width = rows[0].shape[1]
+    return jnp.concatenate((*rows, jnp.zeros((LANES - len(rows), width), jnp.float32))).T
 
 
 def edges_kernel(*refs):
@@ -22,17 +23,18 @@
     pair_ref, gain_ref, shift_ref, lw_ref, lb_ref, rw_ref, rb_ref, gw_ref, gb_ref = vmem
     rows, cols, chans = pair_ref.shape
     hidden = lw_ref.shape[1] // 2
-    for load in loads[:3]:
+    for load in loads:
         load.wait()
-    values = pair_ref[...].reshape(rows * cols, chans).astype(jnp.float32)
-    center = values - jnp.mean(values, axis=1, keepdims=True)
+    pair = pair_ref[...].reshape(rows * cols, chans)
+    share = jnp.full((chans, chans), 1 / chans, jnp.bfloat16)
+    center = pair.astype(jnp.float32) - jnp.dot(pair, share, preferred_element_type=jnp.float32)
     spread = jnp.mean(center * center, axis=1, keepdims=True)
     normed = (center * lax.rsqrt(spread + 1e-05) * gain_ref[...] + shift_ref[...]).astype(jnp.bfloat16)
-    for load in loads[3:]:
-        load.wait()
-    for side, (w_ref, b_ref) in enumerate(((lw_ref, lb_ref), (rw_ref, rb_ref))):
-        gate_bias = column(b_ref[:, :hidden], LANES)[:, :1]
-        value_bias = column(b_ref[:, hidden:], LANES)[:, :1]
+    halves = [ref[:, n : n + hidden] for ref in (lb_ref, rb_ref) for n in (0, hidden)]
+    biases = columns(*halves)
+    for side, w_ref in enumerate((lw_ref, rw_ref)):
+        gate_bias = biases[:, 2 * side : 2 * side + 1]
+        value_bias = biases[:, 2 * side + 1 : 2 * side + 2]
         turned = w_ref[...].T
         for r in range(rows):
             part = normed[r * cols : (r + 1) * cols]
@@ -56,8 +58,8 @@
     center = values - jnp.mean(values, axis=0, keepdims=True)
     spread = jnp.mean(center * center, axis=0, keepdims=True)
     held_ref[...] = (center * lax.rsqrt(spread + 1e-05)).reshape(hidden * subs, lanes)
-    gain = column(gain_ref[...], lanes)
-    shift = column(shift_ref[...], lanes)
+    scale = columns(gain_ref[...], shift_ref[...])
+    gain, shift = scale[:, :1], scale[:, 1:2]
     stores = []
     for s in range(subs):
         mixed = (held_ref[pl.ds(s, hidden, stride=subs), :] * gain + shift).astype(jnp.bfloat16)

time: 171 us -> 171 us (level)
  no operation moved by 1% of the time
where the time goes in v7:
time: 171 us
  blocking collectives  163 us (95%)
  Pallas kernels  3.42 us (2%)
  starting transfers between devices  1.95 us (1%)
    all_to_all x1, blocking collectives, per_device(): got = lax.all_to_all(edges, 'row', split_axis=0, concat_axis=0, tiled=True)  113 us
    all_to_all x1, blocking collectives, per_device(): lax.all_to_all(triangle.reshape(peers, spots // LANES, LANES), 'row', spl...  50.3 us
  transfers between devices with their start and end apart: 1, of which 1 were waited for; matrix products, arithmetic and copies ran while one was open for 0% of the time, Pallas kernels for 0%

profile of v7, /device:TPU:38, one launch (start us, length us, event | category | flops | bytes accessed | tf_op | source)
XLA Modules:
  0.0 170.7 jit_solution(17305479371371106914)
XLA Ops:
  0.0 2.1 %shard_map.127 = (bf16[512,512]{1,0:T(8,128)(2,1)S(1)}, f32[1024,128]{1,0:T(8,128)S(1)}, f32[1,128]{1,0:T(1,128)S(1)}, f32[1,128]{1,0:T(1,128)S(1)}, bf16[128,128]{1,0:T(8,128)(2,1)S(1)}, /*index=5*/f32[1,128]{1,0:T(1,128)S(1)}) custom-call(bf16[4,256,128]{2,1,0:T(8,128)(2,1)} %refs_0_.1, f32[1,128]{1,0:T(1,128)} %bitcast.11, f32[1,128]{1,0:T(1,128)} %bitcast.12, ...), custom_call_target="tpu_custom_call" | custom-call | tf_op jit(solution)/shard_map/pallas_call | solution.py:107
  2.1 0.1 reshape.44
  2.2 112.5 %all_to_all.10 = bf16[128,4,512]{2,1,0:T(4,128)(2,1)S(1)} all-to-all(bf16[128,4,512]{2,1,0:T(4,128)(2,1)S(1)} %reshape.44), channel_id=1, replica_groups=mesh['groups'=2,'row'=128,'col'=2] {'row'}, dimensions={0} | all-to-all | bytes 1048576 | tf_op jit(solution)/shard_map/all_to_all | solution.py:126
  114.8 0.1 reshape.45
  114.9 0.3 convolution_convert_fusion
  115.2 2.0 %collective-permute-start = (bf16[512,256]{1,0:T(8,128)(2,1)S(1)}, bf16[512,256]{1,0:T(8,128)(2,1)S(1)}, u32[]{:S(2)}, u32[]{:S(2)}) collective-permute-start(bf16[512,256]{1,0:T(8,128)(2,1)S(1)} %convolution_convert_fusion), channel_id=1, source_target_pairs={{0,1},{1,0},{2,3},{3,2},{4,5},{5,4},{6,7},{7,6},{8,9},{9,8},{10,11... | collective-permute-start | bytes 786440 | tf_op jit(solution)/shard_map/ppermute | solution.py:136
  117.2 1.5 collective-permute-done
  118.7 0.3 add_convert_fusion
  118.9 0.1 reshape.46
  119.0 50.3 %all_to_all.11.tri_ref = bf16[128,8,128]{2,1,0:T(8,128)(2,1)S(1)} all-to-all(bf16[128,8,128]{2,1,0:T(8,128)(2,1)S(1)} %reshape.46), channel_id=1, replica_groups=mesh['groups'=2,'row'=128,'col'=2] {'row'}, dimensions={0} | all-to-all | bytes 524288 | tf_op jit(solution)/shard_map/all_to_all | solution.py:138
  169.3 1.3 shard_map.128
  (1 shorter events, 0.0 us)
Async XLA Ops:
  115.2 3.5 %collective-permute-start = (bf16[512,256]{1,0:T(8,128)(2,1)S(1)}, bf16[512,256]{1,0:T(8,128)(2,1)S(1)}, u32[]{:S(2)}, u32[]{:S(2)}) collective-permute-start(bf16[512,256]{1,0:T(8,128)(2,1)S(1)} %convolution_convert_fusion), channel_id=1, source_target_pairs={{0,1},{1,0},{2,3},{3,2},{4,5},{5,4},{6,7},{7,6},{8,9},{9,8},{10,11... | collective-permute-start | bytes 786440 | tf_op jit(solution)/shard_map/ppermute | solution.py:136

commit v8 on v7

--- a/solution.py
+++ b/solution.py
@@ -123,9 +123,14 @@
     half = length // halves
     me = lax.axis_index("col").astype(jnp.uint32)
     edges, mine, other = lax.optimization_barrier((edges, me * half, (1 - me) * half))
-    got = lax.all_to_all(edges, "row", split_axis=0, concat_axis=0, tiled=True)
+    first = peers // 4
+    order = [(first + n) % peers for n in range(peers)]
+    got = lax.all_to_all(
+        edges, "row", split_axis=0, concat_axis=0, axis_index_groups=[order], tiled=True
+    )
     got = got.reshape(length, 2 * cols)
-    left, right = got[:, :cols], got[:, cols:]
+    home = (peers - first) * rows
+    left, right = got[:, :cols], jnp.concatenate((got[home:, cols:], got[:home, cols:]))
 
     def partial_sums(start):
         some = lax.dynamic_slice_in_dim(right, start, half, axis=0)
@@ -136,7 +141,8 @@
     away = lax.ppermute(partial_sums(other).astype(jnp.bfloat16), "col", [(0, 1), (1, 0)])
     triangle = (partial_sums(mine) + away.astype(jnp.float32)).astype(jnp.bfloat16)
     triangle = lax.all_to_all(
-        triangle.reshape(peers, spots // LANES, LANES), "row", split_axis=0, concat_axis=0, tiled=True
+        triangle.reshape(peers, spots // LANES, LANES), "row", split_axis=0, concat_axis=0,
+        axis_index_groups=[order], tiled=True,
     )
     update = pl.pallas_call(
         update_kernel,

time: 171 us -> 174 us (1.018); the launches traced: 171 us -> 172 us
  no operation moved by 1% of the time
where the time goes in v8:
time: 174 us; the launch traced here: 172 us
  blocking collectives  164 us (94%)
  Pallas kernels  3.42 us (2%)
  starting transfers between devices  1.95 us (1%)
    all_to_all x1, blocking collectives, per_device(): lax.all_to_all(edges, 'row', split_axis=0, concat_axis=0, axis_index_grou...  114 us
    all_to_all x1, blocking collectives, per_device(): lax.all_to_all(triangle.reshape(peers, spots // LANES, LANES), 'row', spl...  49.6 us
  transfers between devices with their start and end apart: 1, of which 1 were waited for; matrix products, arithmetic and copies ran while one was open for 0% of the time, Pallas kernels for 0%

profile of v8, /device:TPU:38, one launch (start us, length us, event | category | flops | bytes accessed | tf_op | source)
XLA Modules:
  0.0 171.6 jit_solution(9569314326140587257)
XLA Ops:
  0.0 2.1 %shard_map.127 = (bf16[512,512]{1,0:T(8,128)(2,1)S(1)}, f32[1024,128]{1,0:T(8,128)S(1)}, f32[1,128]{1,0:T(1,128)S(1)}, f32[1,128]{1,0:T(1,128)S(1)}, bf16[128,128]{1,0:T(8,128)(2,1)S(1)}, /*index=5*/f32[1,128]{1,0:T(1,128)S(1)}) custom-call(bf16[4,256,128]{2,1,0:T(8,128)(2,1)} %refs_0_.1, f32[1,128]{1,0:T(1,128)} %bitcast.11, f32[1,128]{1,0:T(1,128)} %bitcast.12, ...), custom_call_target="tpu_custom_call" | custom-call | tf_op jit(solution)/shard_map/pallas_call | solution.py:107
  2.1 0.1 reshape.44
  2.2 114.0 %all_to_all.10 = bf16[128,4,512]{2,1,0:T(4,128)(2,1)S(1)} all-to-all(bf16[128,4,512]{2,1,0:T(4,128)(2,1)S(1)} %reshape.44), channel_id=1, replica_groups={{64,66,68,70,72,74,76,78,80,82,84,86,88,90,92,94,96,98,100,102,104,106,..., dimensions={0} | all-to-all | bytes 1048576 | tf_op jit(solution)/shard_map/all_to_all | solution.py:128
  116.3 0.1 reshape.45
  116.4 0.4 convolution_convert_fusion
  116.8 2.0 %collective-permute-start = (bf16[512,256]{1,0:T(8,128)(2,1)S(1)}, bf16[512,256]{1,0:T(8,128)(2,1)S(1)}, u32[]{:S(2)}, u32[]{:S(2)}) collective-permute-start(bf16[512,256]{1,0:T(8,128)(2,1)S(1)} %convolution_convert_fusion), channel_id=1, source_target_pairs={{0,1},{1,0},{2,3},{3,2},{4,5},{5,4},{6,7},{7,6},{8,9},{9,8},{10,11... | collective-permute-start | bytes 786440 | tf_op jit(solution)/shard_map/ppermute | solution.py:141
  118.8 1.5 collective-permute-done
  120.3 0.3 add_convert_fusion
  120.6 0.1 reshape.46
  120.7 49.6 %all_to_all.11.tri_ref = bf16[128,8,128]{2,1,0:T(8,128)(2,1)S(1)} all-to-all(bf16[128,8,128]{2,1,0:T(8,128)(2,1)S(1)} %reshape.46), channel_id=1, replica_groups={{64,66,68,70,72,74,76,78,80,82,84,86,88,90,92,94,96,98,100,102,104,106,..., dimensions={0} | all-to-all | bytes 524288 | tf_op jit(solution)/shard_map/all_to_all | solution.py:143
  170.3 1.3 shard_map.128
  (2 shorter events, 0.0 us)
Async XLA Ops:
  116.8 3.5 %collective-permute-start = (bf16[512,256]{1,0:T(8,128)(2,1)S(1)}, bf16[512,256]{1,0:T(8,128)(2,1)S(1)}, u32[]{:S(2)}, u32[]{:S(2)}) collective-permute-start(bf16[512,256]{1,0:T(8,128)(2,1)S(1)} %convolution_convert_fusion), channel_id=1, source_target_pairs={{0,1},{1,0},{2,3},{3,2},{4,5},{5,4},{6,7},{7,6},{8,9},{9,8},{10,11... | collective-permute-start | bytes 786440 | tf_op jit(solution)/shard_map/ppermute | solution.py:141

commit v9 on v6

--- a/solution.py
+++ b/solution.py
@@ -17,7 +17,7 @@
     hbm, edge_ref, gate_ref, kept, held_ref = refs[:13], refs[13], refs[14], refs[15:19], refs[19]
     vmem, sems = refs[20:29], refs[29]
     loads = [pltpu.make_async_copy(h, v, sems.at[n]) for n, (h, v) in enumerate(zip(hbm, vmem + kept))]
-    for load in loads:
+    for load in loads[: len(vmem)]:
         load.start()
     pair_ref, gain_ref, shift_ref, lw_ref, lb_ref, rw_ref, rb_ref, gw_ref, gb_ref = vmem
     rows, cols, chans = pair_ref.shape
@@ -28,8 +28,10 @@
     center = values - jnp.mean(values, axis=1, keepdims=True)
     spread = jnp.mean(center * center, axis=1, keepdims=True)
     normed = (center * lax.rsqrt(spread + 1e-05) * gain_ref[...] + shift_ref[...]).astype(jnp.bfloat16)
-    for load in loads[3:]:
+    for load in loads[3 : len(vmem)]:
         load.wait()
+    for load in loads[len(vmem) :]:
+        load.start()
     for side, (w_ref, b_ref) in enumerate(((lw_ref, lb_ref), (rw_ref, rb_ref))):
         gate_bias = column(b_ref[:, :hidden], LANES)[:, :1]
         value_bias = column(b_ref[:, hidden:], LANES)[:, :1]
@@ -44,10 +46,13 @@
                 block = (side * cols + at) // LANES
                 held_ref[block, pl.ds(r, hidden, stride=rows), :] = edge[:, at : at + LANES]
     for block in range(held_ref.shape[0]):
-        edge_ref[:, block * LANES : (block + 1) * LANES] = held_ref[block].astype(jnp.bfloat16)
+        turned = held_ref[block].reshape(hidden, rows, LANES)
+        edge_ref[:, :, block * LANES : (block + 1) * LANES] = turned.astype(jnp.bfloat16)
     gate_ref[...] = jax.nn.sigmoid(
         jnp.dot(normed, gw_ref[...], preferred_element_type=jnp.float32) + gb_ref[...]
     )
+    for load in loads[len(vmem) :]:
+        load.wait()
 
 
 def update_kernel(tri_ref, gate_ref, gain_ref, shift_ref, w_ref, b_ref, out_ref, held_ref, made_ref, sems):
@@ -105,7 +110,7 @@
     edges, gate, *closing = pl.pallas_call(
         edges_kernel,
         out_shape=(
-            jax.ShapeDtypeStruct((hidden * rows, 2 * cols), jnp.bfloat16),
+            jax.ShapeDtypeStruct((hidden, rows, 2 * cols), jnp.bfloat16),
             jax.ShapeDtypeStruct((spots, chans), jnp.float32),
             *(jax.ShapeDtypeStruct(v.shape, v.dtype) for v in closing),
         ),
@@ -117,7 +122,6 @@
         ],
         compiler_params=SMALL,
     )(*(pltpu.with_memory_space_constraint(v, pltpu.HBM) for v in (*given, *closing)))
-    edges = edges.reshape(hidden, rows, 2 * cols)
     half = length // halves
     me = lax.axis_index("col").astype(jnp.uint32)
     edges, mine, other = lax.optimization_barrier((edges, me * half, (1 - me) * half))

time: 171 us -> 171 us (level)
  no operation moved by 1% of the time
where the time goes in v9:
time: 171 us
  blocking collectives  163 us (95%)
  Pallas kernels  3.55 us (2%)
  starting transfers between devices  1.95 us (1%)
    all_to_all x1, blocking collectives, per_device(): got = lax.all_to_all(edges, 'row', split_axis=0, concat_axis=0, tiled=True)  113 us
    all_to_all x1, blocking collectives, per_device(): lax.all_to_all(triangle.reshape(peers, spots // LANES, LANES), 'row', spl...  50.3 us
  transfers between devices with their start and end apart: 1, of which 1 were waited for; matrix products, arithmetic and copies ran while one was open for 0% of the time, Pallas kernels for 0%

profile of v9, /device:TPU:38, one launch (start us, length us, event | category | flops | bytes accessed | tf_op | source)
XLA Modules:
  0.0 170.7 jit_solution(1497287006358921400)
XLA Ops:
  0.0 2.2 %shard_map.127 = (bf16[128,4,512]{2,1,0:T(4,128)(2,1)S(1)}, f32[1024,128]{1,0:T(8,128)S(1)}, f32[1,128]{1,0:T(1,128)S(1)}, f32[1,128]{1,0:T(1,128)S(1)}, bf16[12...) custom-call(bf16[4,256,128]{2,1,0:T(8,128)(2,1)} %refs_0_.1, f32[1,128]{1,0:T(1,128)} %bitcast.11, f32[1,128]{1,0:T(1,128)} %bitcast.12, ...), custom_call_target="tpu_custom_call" | custom-call | tf_op jit(solution)/shard_map/pallas_call | solution.py:110
  2.2 112.5 %all_to_all.10 = bf16[128,4,512]{2,1,0:T(4,128)(2,1)S(1)} all-to-all(bf16[128,4,512]{2,1,0:T(4,128)(2,1)S(1)} %get-tuple-element.15), channel_id=1, replica_groups=mesh['groups'=2,'row'=128,'col'=2] {'row'}, dimensions={0} | all-to-all | bytes 1048576 | tf_op jit(solution)/shard_map/all_to_all | solution.py:128
  114.8 0.1 reshape.41
  114.9 0.3 convolution_convert_fusion
  115.2 2.0 %collective-permute-start = (bf16[512,256]{1,0:T(8,128)(2,1)S(1)}, bf16[512,256]{1,0:T(8,128)(2,1)S(1)}, u32[]{:S(2)}, u32[]{:S(2)}) collective-permute-start(bf16[512,256]{1,0:T(8,128)(2,1)S(1)} %convolution_convert_fusion), channel_id=1, source_target_pairs={{0,1},{1,0},{2,3},{3,2},{4,5},{5,4},{6,7},{7,6},{8,9},{9,8},{10,11... | collective-permute-start | bytes 786440 | tf_op jit(solution)/shard_map/ppermute | solution.py:138
  117.2 1.5 collective-permute-done
  118.7 0.3 add_convert_fusion
  118.9 0.1 reshape.42
  119.0 50.3 %all_to_all.11.tri_ref = bf16[128,8,128]{2,1,0:T(8,128)(2,1)S(1)} all-to-all(bf16[128,8,128]{2,1,0:T(8,128)(2,1)S(1)} %reshape.42), channel_id=1, replica_groups=mesh['groups'=2,'row'=128,'col'=2] {'row'}, dimensions={0} | all-to-all | bytes 524288 | tf_op jit(solution)/shard_map/all_to_all | solution.py:140
  169.3 1.3 shard_map.128
  (1 shorter events, 0.0 us)
Async XLA Ops:
  115.2 3.5 %collective-permute-start = (bf16[512,256]{1,0:T(8,128)(2,1)S(1)}, bf16[512,256]{1,0:T(8,128)(2,1)S(1)}, u32[]{:S(2)}, u32[]{:S(2)}) collective-permute-start(bf16[512,256]{1,0:T(8,128)(2,1)S(1)} %convolution_convert_fusion), channel_id=1, source_target_pairs={{0,1},{1,0},{2,3},{3,2},{4,5},{5,4},{6,7},{7,6},{8,9},{9,8},{10,11... | collective-permute-start | bytes 786440 | tf_op jit(solution)/shard_map/ppermute | solution.py:138

commit v10 on v7

--- a/solution.py
+++ b/solution.py
@@ -18,20 +18,23 @@
     hbm, edge_ref, gate_ref, kept, held_ref = refs[:13], refs[13], refs[14], refs[15:19], refs[19]
     vmem, sems = refs[20:29], refs[29]
     loads = [pltpu.make_async_copy(h, v, sems.at[n]) for n, (h, v) in enumerate(zip(hbm, vmem + kept))]
-    for load in loads:
+    for load in loads[: len(vmem)]:
         load.start()
     pair_ref, gain_ref, shift_ref, lw_ref, lb_ref, rw_ref, rb_ref, gw_ref, gb_ref = vmem
     rows, cols, chans = pair_ref.shape
     hidden = lw_ref.shape[1] // 2
-    for load in loads:
+    for load in loads[:3]:
         load.wait()
     pair = pair_ref[...].reshape(rows * cols, chans)
     share = jnp.full((chans, chans), 1 / chans, jnp.bfloat16)
     center = pair.astype(jnp.float32) - jnp.dot(pair, share, preferred_element_type=jnp.float32)
     spread = jnp.mean(center * center, axis=1, keepdims=True)
     normed = (center * lax.rsqrt(spread + 1e-05) * gain_ref[...] + shift_ref[...]).astype(jnp.bfloat16)
-    halves = [ref[:, n : n + hidden] for ref in (lb_ref, rb_ref) for n in (0, hidden)]
-    biases = columns(*halves)
+    for load in loads[3 : len(vmem)]:
+        load.wait()
+    for load in loads[len(vmem) :]:
+        load.start()
+    biases = columns(*(ref[:, n : n + hidden] for ref in (lb_ref, rb_ref) for n in (0, hidden)))
     for side, w_ref in enumerate((lw_ref, rw_ref)):
         gate_bias = biases[:, 2 * side : 2 * side + 1]
         value_bias = biases[:, 2 * side + 1 : 2 * side + 2]
@@ -46,10 +49,13 @@
                 block = (side * cols + at) // LANES
                 held_ref[block, pl.ds(r, hidden, stride=rows), :] = edge[:, at : at + LANES]
     for block in range(held_ref.shape[0]):
-        edge_ref[:, block * LANES : (block + 1) * LANES] = held_ref[block].astype(jnp.bfloat16)
+        turned = held_ref[block].reshape(hidden, rows, LANES)
+        edge_ref[:, :, block * LANES : (block + 1) * LANES] = turned.astype(jnp.bfloat16)
     gate_ref[...] = jax.nn.sigmoid(
         jnp.dot(normed, gw_ref[...], preferred_element_type=jnp.float32) + gb_ref[...]
     )
+    for load in loads[len(vmem) :]:
+        load.wait()
 
 
 def update_kernel(tri_ref, gate_ref, gain_ref, shift_ref, w_ref, b_ref, out_ref, held_ref, made_ref, sems):
@@ -107,7 +113,7 @@
     edges, gate, *closing = pl.pallas_call(
         edges_kernel,
         out_shape=(
-            jax.ShapeDtypeStruct((hidden * rows, 2 * cols), jnp.bfloat16),
+            jax.ShapeDtypeStruct((hidden, rows, 2 * cols), jnp.bfloat16),
             jax.ShapeDtypeStruct((spots, chans), jnp.float32),
             *(jax.ShapeDtypeStruct(v.shape, v.dtype) for v in closing),
         ),
@@ -119,7 +125,6 @@
         ],
         compiler_params=SMALL,
     )(*(pltpu.with_memory_space_constraint(v, pltpu.HBM) for v in (*given, *closing)))
-    edges = edges.reshape(hidden, rows, 2 * cols)
     half = length // halves
     me = lax.axis_index("col").astype(jnp.uint32)
     edges, mine, other = lax.optimization_barrier((edges, me * half, (1 - me) * half))

time: 171 us -> 171 us (level)
  no operation moved by 1% of the time
where the time goes in v10:
time: 171 us
  blocking collectives  163 us (95%)
  Pallas kernels  3.59 us (2%)
  starting transfers between devices  1.95 us (1%)
    all_to_all x1, blocking collectives, per_device(): got = lax.all_to_all(edges, 'row', split_axis=0, concat_axis=0, tiled=True)  113 us
    all_to_all x1, blocking collectives, per_device(): lax.all_to_all(triangle.reshape(peers, spots // LANES, LANES), 'row', spl...  50.3 us
  transfers between devices with their start and end apart: 1, of which 1 were waited for; matrix products, arithmetic and copies ran while one was open for 0% of the time, Pallas kernels for 0%

profile of v10, /device:TPU:38, one launch (start us, length us, event | category | flops | bytes accessed | tf_op | source)
XLA Modules:
  0.0 170.7 jit_solution(7540614364591290736)
XLA Ops:
  0.0 2.2 %shard_map.127 = (bf16[128,4,512]{2,1,0:T(4,128)(2,1)S(1)}, f32[1024,128]{1,0:T(8,128)S(1)}, f32[1,128]{1,0:T(1,128)S(1)}, f32[1,128]{1,0:T(1,128)S(1)}, bf16[12...) custom-call(bf16[4,256,128]{2,1,0:T(8,128)(2,1)} %refs_0_.1, f32[1,128]{1,0:T(1,128)} %bitcast.11, f32[1,128]{1,0:T(1,128)} %bitcast.12, ...), custom_call_target="tpu_custom_call" | custom-call | tf_op jit(solution)/shard_map/pallas_call | solution.py:113
  2.3 112.5 %all_to_all.10 = bf16[128,4,512]{2,1,0:T(4,128)(2,1)S(1)} all-to-all(bf16[128,4,512]{2,1,0:T(4,128)(2,1)S(1)} %get-tuple-element.15), channel_id=1, replica_groups=mesh['groups'=2,'row'=128,'col'=2] {'row'}, dimensions={0} | all-to-all | bytes 1048576 | tf_op jit(solution)/shard_map/all_to_all | solution.py:131
  114.8 0.1 reshape.41
  114.9 0.3 convolution_convert_fusion
  115.2 2.0 %collective-permute-start = (bf16[512,256]{1,0:T(8,128)(2,1)S(1)}, bf16[512,256]{1,0:T(8,128)(2,1)S(1)}, u32[]{:S(2)}, u32[]{:S(2)}) collective-permute-start(bf16[512,256]{1,0:T(8,128)(2,1)S(1)} %convolution_convert_fusion), channel_id=1, source_target_pairs={{0,1},{1,0},{2,3},{3,2},{4,5},{5,4},{6,7},{7,6},{8,9},{9,8},{10,11... | collective-permute-start | bytes 786440 | tf_op jit(solution)/shard_map/ppermute | solution.py:141
  117.2 1.5 collective-permute-done
  118.7 0.3 add_convert_fusion
  118.9 0.1 reshape.42
  119.0 50.3 %all_to_all.11.tri_ref = bf16[128,8,128]{2,1,0:T(8,128)(2,1)S(1)} all-to-all(bf16[128,8,128]{2,1,0:T(8,128)(2,1)S(1)} %reshape.42), channel_id=1, replica_groups=mesh['groups'=2,'row'=128,'col'=2] {'row'}, dimensions={0} | all-to-all | bytes 524288 | tf_op jit(solution)/shard_map/all_to_all | solution.py:143
  169.3 1.3 shard_map.128
  (1 shorter events, 0.0 us)
Async XLA Ops:
  115.2 3.5 %collective-permute-start = (bf16[512,256]{1,0:T(8,128)(2,1)S(1)}, bf16[512,256]{1,0:T(8,128)(2,1)S(1)}, u32[]{:S(2)}, u32[]{:S(2)}) collective-permute-start(bf16[512,256]{1,0:T(8,128)(2,1)S(1)} %convolution_convert_fusion), channel_id=1, source_target_pairs={{0,1},{1,0},{2,3},{3,2},{4,5},{5,4},{6,7},{7,6},{8,9},{9,8},{10,11... | collective-permute-start | bytes 786440 | tf_op jit(solution)/shard_map/ppermute | solution.py:141
